TPU v7x, 32 devices: a whole 2x2x4 slice. The times are simulated.
32 devices in a mesh: tok: 8 (over z, y), vocab: 4 (over x, core).
Axes of the slice: x: 2, y: 2, z: 4, core: 2. Of those that a mesh axis runs over, the one named last changes fastest.
Arguments:
- hidden: bfloat16 [192, 9216], P('tok'), may hold values from -256 to 256
- policy_head: bfloat16 [9216, 32768], P(None, ('tok', 'vocab')), may hold values from -0.0625 to 0.0625
- reference_head: bfloat16 [9216, 32768], P(None, ('tok', 'vocab')), may hold values from -0.0625 to 0.0625
- targets: int32 [192], P('tok'), may hold values from 0 to 32767
Outputs:
- policy_logprob: float32 [192], P('tok')
- reference_logprob: float32 [192], P('tok')
- divergence: float32 [192], P('tok')
All inputs are finite; a program needn't handle non-finite values.
Results may differ from a plain program's by a relative error of at most 0.00055.
Values may be sent and summed in bfloat16 or wider, within the bound.
A program may use at most 128 MiB of HBM per device.

v0:
```python
import jax
import jax.numpy as jnp
from jax import lax
from jax.sharding import PartitionSpec as P


def combined_all(value, axis, combine):
    everything = jax.tree.map(lambda part: lax.all_gather(part, axis), value)
    leading = jax.tree.map(lambda part: part[0], everything)

    def step(k, so_far):
        return combine(so_far, jax.tree.map(lambda part: part[k], everything))

    return lax.fori_loop(1, lax.axis_size(axis), step, leading)


def local_sums(policy_logits, reference_logits, target_hits, peak_policy, peak_reference):
    policy_exp = jnp.exp(policy_logits - peak_policy[:, None])
    reference_exp = jnp.exp(reference_logits - peak_reference[:, None])
    total_policy = jnp.sum(policy_exp, axis=1)
    total_reference = jnp.sum(reference_exp, axis=1)
    weighted = jnp.sum(policy_exp * (policy_logits - reference_logits), axis=1)
    target_policy = jnp.sum(jnp.where(target_hits, policy_logits, 0.0), axis=1)
    target_reference = jnp.sum(jnp.where(target_hits, reference_logits, 0.0), axis=1)
    return (total_policy, total_reference, weighted, target_policy, target_reference)


def local_stats(policy_logits, reference_logits, target_hits):
    peak_policy = jnp.max(policy_logits, axis=1)
    peak_reference = jnp.max(reference_logits, axis=1)
    summed = local_sums(policy_logits, reference_logits, target_hits, peak_policy, peak_reference)
    return (peak_policy, peak_reference) + summed


def combine_stats(left_stats, right_stats):
    peak_policy = jnp.maximum(left_stats[0], right_stats[0])
    peak_reference = jnp.maximum(left_stats[1], right_stats[1])
    left_policy = jnp.exp(left_stats[0] - peak_policy)
    right_policy = jnp.exp(right_stats[0] - peak_policy)
    left_reference = jnp.exp(left_stats[1] - peak_reference)
    right_reference = jnp.exp(right_stats[1] - peak_reference)
    return (
        peak_policy,
        peak_reference,
        left_stats[2] * left_policy + right_stats[2] * right_policy,
        left_stats[3] * left_reference + right_stats[3] * right_reference,
        left_stats[4] * left_policy + right_stats[4] * right_policy,
        left_stats[5] + right_stats[5],
        left_stats[6] + right_stats[6],
    )


def combine_senders(received):
    peak_policy = jnp.max(received[0], axis=0)
    peak_reference = jnp.max(received[1], axis=0)
    policy_scale = jnp.exp(received[0] - peak_policy[None, :])
    reference_scale = jnp.exp(received[1] - peak_reference[None, :])
    return (
        peak_policy,
        peak_reference,
        jnp.sum(received[2] * policy_scale, axis=0),
        jnp.sum(received[3] * reference_scale, axis=0),
        jnp.sum(received[4] * policy_scale, axis=0),
        jnp.sum(received[5], axis=0),
        jnp.sum(received[6], axis=0),
    )


def finish(merged_stats):
    log_norm_policy = merged_stats[0] + jnp.log(merged_stats[2])
    log_norm_reference = merged_stats[1] + jnp.log(merged_stats[3])
    policy_logprob = merged_stats[5] - log_norm_policy
    reference_logprob = merged_stats[6] - log_norm_reference
    divergence = merged_stats[4] / merged_stats[2] - log_norm_policy + log_norm_reference
    return (policy_logprob, reference_logprob, divergence)


def body(hidden, policy_head, reference_head, targets):
    tok_count = lax.axis_size("tok")
    vocab_count = lax.axis_size("vocab")
    tok_rows = hidden.shape[0]
    vocab_cols = policy_head.shape[1]
    piece = lax.all_gather(hidden, "tok", axis=0, tiled=True)
    summed = jnp.concatenate(
        [
            jnp.dot(piece, policy_head, preferred_element_type=jnp.float32),
            jnp.dot(piece, reference_head, preferred_element_type=jnp.float32),
        ],
        axis=1,
    )
    policy_logits = summed[:, :vocab_cols]
    reference_logits = summed[:, vocab_cols:]
    every_target = lax.all_gather(targets, "tok", axis=0, tiled=True)
    block_index = lax.axis_index("tok") * vocab_count + lax.axis_index("vocab")
    vocab_ids = block_index * vocab_cols + lax.iota(jnp.int32, vocab_cols)
    target_hits = vocab_ids[None, :] == every_target[:, None]
    partial_value = local_stats(policy_logits, reference_logits, target_hits)
    shaped = tuple((entry.reshape(tok_count, tok_rows) for entry in partial_value))
    received = lax.all_to_all(shaped, "tok", split_axis=0, concat_axis=0, tiled=True)
    own_stats = combine_senders(received)
    merged_stats = combined_all(own_stats, "vocab", combine_stats)
    return finish(merged_stats)


def solution(mesh):
    in_specs = (P("tok", None), P(None, ("tok", "vocab")), P(None, ("tok", "vocab")), P("tok"))
    out_specs = (P("tok"), P("tok"), P("tok"))
    return jax.shard_map(body, mesh=mesh, in_specs=in_specs, out_specs=out_specs, check_vma=False)
```

profile of v0, /device:TPU:0, one launch (start us, length us, event | category | flops | bytes accessed | tf_op | source)
XLA Modules:
  0.0 179.8 jit_solution(15287167651976823062)
XLA Ops:
  7.2 0.0 all-gather.9.cloned.1.call-start
  7.2 0.7 all-gather.9.cloned.1.call-update
  7.9 1.2 dynamic-slice.5
  9.8 0.9 dynamic-update-slice.5
  10.7 13.1 %all-reduce.5 = s32[192]{0:T(256)S(1)} all-reduce(s32[192]{0:T(256)S(1)} %dynamic-update-slice.5), channel_id=1, replica_groups=mesh['tok'=8,'vocab'=4] {'tok'}, use_global_device_ids=true, to_apply=%add.5 | all-reduce | flops 192 | bytes 1536
  23.8 53.8 %all-gather.9.cloned.1.call-done = bf16[192,9216]{1,0:T(8,128)(2,1)} async-done(((bf16[24,9216]{1,0:T(8,128)(2,1)}), bf16[192,9216]{1,0:T(8,128)(2,1)}) %all-gather.9.cloned.1.call-update) | async-done | bytes 3538960 | tf_op jit(solution)/shard_map/all_gather | solution.py:83
  77.5 0.0 copy-start
  77.5 9.6 %fusion.24 = (f32[192]{0:T(256)S(1)}, f32[192,1024]{1,0:T(8,128)S(1)}) fusion(bf16[192,9216]{1,0:T(8,128)(2,1)} %all-gather.9.cloned.1.call-done, bf16[9216,1024]{1,0:T(8,128)(2,1)} %param.7), kind=kOutput, calls=%fused_computation.44 | convolution fusion | flops 3624075008 | bytes 23200512 | tf_op jit(solution)/shard_map/dot_general | solution.py:86
  87.2 3.1 %copy-done = bf16[9216,1024]{1,0:T(8,128)(2,1)S(1)} copy-done((bf16[9216,1024]{1,0:T(8,128)(2,1)S(1)}, bf16[9216,1024]{1,0:T(8,128)(2,1)}, u32[]{:S(2)}) %copy-start) | copy-done | bytes 18874392
  90.3 0.0 copy-start.1
  90.3 5.9 %fusion.25 = (f32[192]{0:T(256)S(1)}, f32[192,1024]{1,0:T(8,128)S(1)}) fusion(bf16[192,9216]{1,0:T(8,128)(2,1)} %all-gather.9.cloned.1.call-done, bf16[9216,1024]{1,0:T(8,128)(2,1)S(1)} %copy-done), kind=kOutput, calls=%fused_computation.45 | convolution fusion | flops 3624075008 | bytes 23200512 | tf_op jit(solution)/shard_map/dot_general | solution.py:87
  96.2 0.7 multiply_reduce_fusion
  96.9 0.7 all_to_all.64
  97.5 3.3 %all-to-all-start.4 = ((f32[8,1,24]{2,1,0:T(1,128)}), f32[8,1,24]{2,1,0:T(1,128)S(1)}, u32[]{:S(2)}, u32[]{:S(2)}) async-start(f32[8,1,24]{2,1,0:T(1,128)} %all_to_all.64), calls=%async_computation.4 | async-start | bytes 8192 | tf_op jit(solution)/shard_map/all_to_all | solution.py:99
  100.9 0.7 all_to_all.56
  101.6 5.8 %all-to-all-done.4 = f32[8,1,24]{2,1,0:T(1,128)S(1)} async-done(((f32[8,1,24]{2,1,0:T(1,128)}), f32[8,1,24]{2,1,0:T(1,128)S(1)}, u32[]{:S(2)}, u32[]{:S(2)}) %all-to-all-start.4) | async-done | bytes 800 | tf_op jit(solution)/shard_map/all_to_all | solution.py:99
  107.4 3.2 %all-to-all-start.2 = ((f32[8,1,24]{2,1,0:T(1,128)}), f32[8,1,24]{2,1,0:T(1,128)S(1)}, u32[]{:S(2)}, u32[]{:S(2)}) async-start(f32[8,1,24]{2,1,0:T(1,128)} %all_to_all.56), calls=%async_computation.2 | async-start | bytes 8192 | tf_op jit(solution)/shard_map/all_to_all | solution.py:99
  110.6 0.7 all_to_all.52
  111.3 5.7 %all-to-all-done.2 = f32[8,1,24]{2,1,0:T(1,128)S(1)} async-done(((f32[8,1,24]{2,1,0:T(1,128)}), f32[8,1,24]{2,1,0:T(1,128)S(1)}, u32[]{:S(2)}, u32[]{:S(2)}) %all-to-all-start.2) | async-done | bytes 800 | tf_op jit(solution)/shard_map/all_to_all | solution.py:99
  117.1 3.3 %all-to-all-start = ((f32[8,1,24]{2,1,0:T(1,128)}), f32[8,1,24]{2,1,0:T(1,128)S(1)}, u32[]{:S(2)}, u32[]{:S(2)}) async-start(f32[8,1,24]{2,1,0:T(1,128)} %all_to_all.52), calls=%async_computation | async-start | bytes 8192 | tf_op jit(solution)/shard_map/all_to_all | solution.py:99
  120.4 0.7 all_to_all.60
  121.1 5.8 %all-to-all-done = f32[8,1,24]{2,1,0:T(1,128)S(1)} async-done(((f32[8,1,24]{2,1,0:T(1,128)}), f32[8,1,24]{2,1,0:T(1,128)S(1)}, u32[]{:S(2)}, u32[]{:S(2)}) %all-to-all-start) | async-done | bytes 800 | tf_op jit(solution)/shard_map/all_to_all | solution.py:99
  126.8 3.2 %all-to-all-start.3 = ((f32[8,1,24]{2,1,0:T(1,128)}), f32[8,1,24]{2,1,0:T(1,128)S(1)}, u32[]{:S(2)}, u32[]{:S(2)}) async-start(f32[8,1,24]{2,1,0:T(1,128)} %all_to_all.60), calls=%async_computation.3 | async-start | bytes 8192 | tf_op jit(solution)/shard_map/all_to_all | solution.py:99
  130.1 0.7 all_to_all.54
  130.8 5.7 %all-to-all-done.3 = f32[8,1,24]{2,1,0:T(1,128)S(1)} async-done(((f32[8,1,24]{2,1,0:T(1,128)}), f32[8,1,24]{2,1,0:T(1,128)S(1)}, u32[]{:S(2)}, u32[]{:S(2)}) %all-to-all-start.3) | async-done | bytes 800 | tf_op jit(solution)/shard_map/all_to_all | solution.py:99
  136.5 3.3 %all-to-all-start.1 = ((f32[8,1,24]{2,1,0:T(1,128)}), f32[8,1,24]{2,1,0:T(1,128)S(1)}, u32[]{:S(2)}, u32[]{:S(2)}) async-start(f32[8,1,24]{2,1,0:T(1,128)} %all_to_all.54), calls=%async_computation.1 | async-start | bytes 8192 | tf_op jit(solution)/shard_map/all_to_all | solution.py:99
  139.9 0.0 copy-done.1
  139.9 0.6 dynamic-slice
  141.1 0.7 all_to_all.67
  141.8 0.7 all_to_all.69
  142.5 3.8 %all-to-all-done.1 = f32[8,1,24]{2,1,0:T(1,128)S(1)} async-done(((f32[8,1,24]{2,1,0:T(1,128)}), f32[8,1,24]{2,1,0:T(1,128)S(1)}, u32[]{:S(2)}, u32[]{:S(2)}) %all-to-all-start.1) | async-done | bytes 800 | tf_op jit(solution)/shard_map/all_to_all | solution.py:99
  146.3 3.2 %all-to-all-start.5 = ((f32[8,1,24]{2,1,0:T(1,128)}), f32[8,1,24]{2,1,0:T(1,128)S(1)}, u32[]{:S(2)}, u32[]{:S(2)}) async-start(f32[8,1,24]{2,1,0:T(1,128)} %all_to_all.67), calls=%async_computation.5 | async-start | bytes 8192 | tf_op jit(solution)/shard_map/all_to_all | solution.py:99
  149.6 6.4 %all-to-all-done.5 = f32[8,1,24]{2,1,0:T(1,128)S(1)} async-done(((f32[8,1,24]{2,1,0:T(1,128)}), f32[8,1,24]{2,1,0:T(1,128)S(1)}, u32[]{:S(2)}, u32[]{:S(2)}) %all-to-all-start.5) | async-done | bytes 800 | tf_op jit(solution)/shard_map/all_to_all | solution.py:99
  156.0 3.3 %all-to-all-start.6 = ((f32[8,1,24]{2,1,0:T(1,128)}), f32[8,1,24]{2,1,0:T(1,128)S(1)}, u32[]{:S(2)}, u32[]{:S(2)}) async-start(f32[8,1,24]{2,1,0:T(1,128)} %all_to_all.69), calls=%async_computation.6 | async-start | bytes 8192 | tf_op jit(solution)/shard_map/all_to_all | solution.py:99
  159.3 0.2 dynamic-update-slice
  159.5 0.2 dynamic-update-slice.1
  159.7 0.2 dynamic-update-slice.4
  159.9 0.2 dynamic-update-slice.2
  160.1 0.2 dynamic-update-slice.3
  160.4 0.2 dynamic-update-slice.6
  160.6 5.1 %all-to-all-done.6 = f32[8,1,24]{2,1,0:T(1,128)S(1)} async-done(((f32[8,1,24]{2,1,0:T(1,128)}), f32[8,1,24]{2,1,0:T(1,128)S(1)}, u32[]{:S(2)}, u32[]{:S(2)}) %all-to-all-start.6) | async-done | bytes 800 | tf_op jit(solution)/shard_map/all_to_all | solution.py:99
  165.7 0.2 dynamic-update-slice.7
  165.9 5.6 %all-reduce.8 = (f32[96]{0:T(128)S(1)}, f32[96]{0:T(128)S(1)}, f32[96]{0:T(128)S(1)}, f32[96]{0:T(128)S(1)}, f32[96]{0:T(128)S(1)}, /*index=5*/f32[96]{0:T(128)S(1)}, f32[96]{0:T(128)S(1)}) all-reduce(f32[96]{0:T(128)S(1)} %dynamic-update-slice, f32[96]{0:T(128)S(1)} %dynamic-update-slice.1, ...), channel_id=2, replica_groups=mesh['tok'=8,'vocab'=4] {'vocab'}, use_global_device_ids=true, to_apply=%add | all-reduce | flops 672 | bytes 5376
  171.6 0.1 reshape.43
  171.7 0.1 reshape.44
  171.7 0.1 reshape.45
  171.8 0.1 reshape.46
  171.9 0.1 reshape.47
  172.0 0.1 reshape.48
  172.1 0.1 reshape.49
  172.2 0.3 while.27
  172.5 0.5 subtract_add_fusion
  (27 shorter events, 0.4 us)
Async XLA Ops:
  7.2 70.3 %all-gather.9.cloned.1.call-start = ((), (), s32[]{:S(2)}) async-start(), calls=%async_computation.7 | async-start | bytes 3981312 | tf_op jit(solution)/shard_map/all_gather | solution.py:83
  77.5 12.7 %copy-start = (bf16[9216,1024]{1,0:T(8,128)(2,1)S(1)}, bf16[9216,1024]{1,0:T(8,128)(2,1)}, u32[]{:S(2)}) copy-start(bf16[9216,1024]{1,0:T(8,128)(2,1)} %param.8) | copy-start | bytes 56623108
  90.3 49.6 %copy-start.1 = (u32[32]{0:T(128)S(1)}, u32[32]{0:T(128)}, u32[]{:S(2)}) copy-start(u32[32]{0:T(128)} %constant.57) | copy-start | bytes 388
  97.5 9.8 %all-to-all-start.4 = ((f32[8,1,24]{2,1,0:T(1,128)}), f32[8,1,24]{2,1,0:T(1,128)S(1)}, u32[]{:S(2)}, u32[]{:S(2)}) async-start(f32[8,1,24]{2,1,0:T(1,128)} %all_to_all.64), calls=%async_computation.4 | async-start | bytes 8192 | tf_op jit(solution)/shard_map/all_to_all | solution.py:99
  107.4 9.7 %all-to-all-start.2 = ((f32[8,1,24]{2,1,0:T(1,128)}), f32[8,1,24]{2,1,0:T(1,128)S(1)}, u32[]{:S(2)}, u32[]{:S(2)}) async-start(f32[8,1,24]{2,1,0:T(1,128)} %all_to_all.56), calls=%async_computation.2 | async-start | bytes 8192 | tf_op jit(solution)/shard_map/all_to_all | solution.py:99
  117.1 9.8 %all-to-all-start = ((f32[8,1,24]{2,1,0:T(1,128)}), f32[8,1,24]{2,1,0:T(1,128)S(1)}, u32[]{:S(2)}, u32[]{:S(2)}) async-start(f32[8,1,24]{2,1,0:T(1,128)} %all_to_all.52), calls=%async_computation | async-start | bytes 8192 | tf_op jit(solution)/shard_map/all_to_all | solution.py:99
  126.8 9.7 %all-to-all-start.3 = ((f32[8,1,24]{2,1,0:T(1,128)}), f32[8,1,24]{2,1,0:T(1,128)S(1)}, u32[]{:S(2)}, u32[]{:S(2)}) async-start(f32[8,1,24]{2,1,0:T(1,128)} %all_to_all.60), calls=%async_computation.3 | async-start | bytes 8192 | tf_op jit(solution)/shard_map/all_to_all | solution.py:99
  136.5 9.8 %all-to-all-start.1 = ((f32[8,1,24]{2,1,0:T(1,128)}), f32[8,1,24]{2,1,0:T(1,128)S(1)}, u32[]{:S(2)}, u32[]{:S(2)}) async-start(f32[8,1,24]{2,1,0:T(1,128)} %all_to_all.54), calls=%async_computation.1 | async-start | bytes 8192 | tf_op jit(solution)/shard_map/all_to_all | solution.py:99
  146.3 9.7 %all-to-all-start.5 = ((f32[8,1,24]{2,1,0:T(1,128)}), f32[8,1,24]{2,1,0:T(1,128)S(1)}, u32[]{:S(2)}, u32[]{:S(2)}) async-start(f32[8,1,24]{2,1,0:T(1,128)} %all_to_all.67), calls=%async_computation.5 | async-start | bytes 8192 | tf_op jit(solution)/shard_map/all_to_all | solution.py:99
  156.0 9.7 %all-to-all-start.6 = ((f32[8,1,24]{2,1,0:T(1,128)}), f32[8,1,24]{2,1,0:T(1,128)S(1)}, u32[]{:S(2)}, u32[]{:S(2)}) async-start(f32[8,1,24]{2,1,0:T(1,128)} %all_to_all.69), calls=%async_computation.6 | async-start | bytes 8192 | tf_op jit(solution)/shard_map/all_to_all | solution.py:99
Sparse Core Ops, SparseCore 0:
  10.2 67.3 all-gather.8
where the time goes:
time: 180 us
  waiting for transfers between devices  92.7 us (52%)
  starting transfers between devices  23.1 us (13%)
  blocking collectives  18.7 us (10%)
  matrix products  15.6 us (9%)
  between operations  15.5 us (9%)
  local copies, waits for them, and re-layouts  12.7 us (7%)
    all_gather x1, waiting for transfers between devices, body(): piece = lax.all_gather(hidden, 'tok', axis=0, tiled=True)  53.8 us
    all_to_all x7, waiting for transfers between devices, body(): lax.all_to_all(shaped, 'tok', split_axis=0, concat_axis=0, tiled=True)  38.3 us
    all_to_all x7, starting transfers between devices, body(): lax.all_to_all(shaped, 'tok', split_axis=0, concat_axis=0, tiled=True)  23 us
    unnamed x2, blocking collectives  18.7 us
    dot_general x1, matrix products, body(): jnp.dot(piece, policy_head, preferred_element_type=jnp.float32)  9.63 us
    unnamed x22, local copies, waits for them, and re-layouts  7.34 us
    dot_general x1, matrix products, body(): jnp.dot(piece, reference_head, preferred_element_type=jnp.float32)  5.92 us
    all_to_all x7, local copies, waits for them, and re-layouts, body(): lax.all_to_all(shaped, 'tok', split_axis=0, concat_axis=0, tiled=True)  4.75 us
  transfers between devices with their start and end apart: 8, of which 8 were waited for; matrix products, arithmetic and copies ran while one was open for 2% of the time, Pallas kernels for 0%

commit v1 on v0

--- a/solution.py
+++ b/solution.py
@@ -80,7 +80,21 @@
     vocab_count = lax.axis_size("vocab")
     tok_rows = hidden.shape[0]
     vocab_cols = policy_head.shape[1]
-    piece = lax.all_gather(hidden, "tok", axis=0, tiled=True)
+
+    def treat_state(mine):
+        devs = lax.axis_size("tok")
+        buffer = [mine]
+        for it in range(1, devs):
+            buffer.append(
+                lax.ppermute(
+                    buffer[it - 1],
+                    axis_name="tok",
+                    perm=[(pp, (pp - 1) % devs) for pp in range(devs)],
+                )
+            )
+        return jnp.roll(jnp.concatenate(buffer, 0), lax.axis_index("tok") * mine.shape[0], 0)
+
+    piece = treat_state(hidden)
     summed = jnp.concatenate(
         [
             jnp.dot(piece, policy_head, preferred_element_type=jnp.float32),

time: 180 us -> 195 us (1.083)
  starting transfers between devices: 23.1 us -> 57.8 us
  waiting for transfers between devices: 92.7 us -> 75.2 us
  between operations: 15.5 us -> 2.09 us
  local copies, waits for them, and re-layouts: 12.7 us -> 23.4 us
  matrix products: 15.6 us -> 18.2 us
  blocking collectives: 18.7 us -> 16.1 us
    all_gather x1 -> x0, waiting for transfers between devices: 53.8 us -> none  [body(): piece = lax.all_gather(hidden, 'tok', axis=0, tiled=True)]
    ppermute x0 -> x7, waiting for transfers between devices: none -> 36.9 us  [treat_state(): lax.ppermute(buffer[it - 1], axis_name='tok', perm=[(pp, (pp - 1) % devs)...]
    ppermute x0 -> x7, starting transfers between devices: none -> 31.6 us  [treat_state(): lax.ppermute(buffer[it - 1], axis_name='tok', perm=[(pp, (pp - 1) % devs)...]
    unnamed x22 -> x39, local copies, waits for them, and re-layouts: 7.34 us -> 17.3 us
    dot_general x1, matrix products: 5.92 us -> 9.63 us  [body(): jnp.dot(piece, reference_head, preferred_element_type=jnp.float32)]
    all_to_all x7, starting transfers between devices: 23 us -> 26.2 us  [body(): lax.all_to_all(shaped, 'tok', split_axis=0, concat_axis=0, tiled=True)]
    unnamed x2, blocking collectives: 18.7 us -> 16.1 us
  transfers between devices with their start and end apart: 8 -> 14, of which waited for: 8 -> 13; matrix products, arithmetic and copies ran while one was open for 2% -> 6% of each run, Pallas kernels for 0% -> 0%
where the time goes in v1:
time: 195 us
  waiting for transfers between devices  75.2 us (39%)
  starting transfers between devices  57.8 us (30%)
  local copies, waits for them, and re-layouts  23.4 us (12%)
  matrix products  18.2 us (9%)
  blocking collectives  16.1 us (8%)
  between operations  2.09 us (1%)
    all_to_all x7, waiting for transfers between devices, body(): lax.all_to_all(shaped, 'tok', split_axis=0, concat_axis=0, tiled=True)  38.3 us
    ppermute x7, waiting for transfers between devices, treat_state(): lax.ppermute(buffer[it - 1], axis_name='tok', perm=[(pp, (pp - 1) % devs)...  36.9 us
    ppermute x7, starting transfers between devices, treat_state(): lax.ppermute(buffer[it - 1], axis_name='tok', perm=[(pp, (pp - 1) % devs)...  31.6 us
    all_to_all x7, starting transfers between devices, body(): lax.all_to_all(shaped, 'tok', split_axis=0, concat_axis=0, tiled=True)  26.2 us
    unnamed x39, local copies, waits for them, and re-layouts  17.3 us
    unnamed x2, blocking collectives  16.1 us
    dot_general x1, matrix products, body(): jnp.dot(piece, reference_head, preferred_element_type=jnp.float32)  9.63 us
    dot_general x1, matrix products, body(): jnp.dot(piece, policy_head, preferred_element_type=jnp.float32)  8.61 us
  transfers between devices with their start and end apart: 14, of which 13 were waited for; matrix products, arithmetic and copies ran while one was open for 6% of the time, Pallas kernels for 0%

profile of v1, /device:TPU:0, one launch (start us, length us, event | category | flops | bytes accessed | tf_op | source)
XLA Modules:
  0.0 194.6 jit_solution(13074831542316297697)
XLA Ops:
  0.6 6.1 %collective-permute-start = (bf16[24,9216]{1,0:T(8,128)(2,1)}, bf16[24,9216]{1,0:T(8,128)(2,1)S(1)}, u32[]{:S(2)}, u32[]{:S(2)}) collective-permute-start(bf16[24,9216]{1,0:T(8,128)(2,1)} %param.6), channel_id=1, source_target_pairs={{0,28},{4,0},{8,4},{12,8},{16,12},{20,16},{24,20},{28,24},{1,29},{... | collective-permute-start | bytes 1327112 | tf_op jit(solution)/shard_map/ppermute | solution.py:89
  6.7 1.8 constant_dynamic-update-slice_fusion.15
  8.6 1.2 dynamic-slice.5
  10.5 0.9 dynamic-update-slice.5
  11.3 10.4 %all-reduce.5 = s32[192]{0:T(256)S(1)} all-reduce(s32[192]{0:T(256)S(1)} %dynamic-update-slice.5), channel_id=1, replica_groups=mesh['tok'=8,'vocab'=4] {'tok'}, use_global_device_ids=true, to_apply=%add.5 | all-reduce | flops 192 | bytes 1536
  21.8 1.2 collective-permute-start.1
  23.0 0.8 constant_dynamic-update-slice_fusion.14
  23.8 8.3 %collective-permute-done.1 = bf16[24,9216]{1,0:T(8,128)(2,1)S(1)} collective-permute-done((bf16[24,9216]{1,0:T(8,128)(2,1)S(1)}, bf16[24,9216]{1,0:T(8,128)(2,1)S(1)}, u32[]{:S(2)}, u32[]{:S(2)}) %collective-permute-start.1) | collective-permute-done | bytes 442400 | tf_op jit(solution)/shard_map/ppermute | solution.py:89
  32.1 3.6 %collective-permute-start.2 = (bf16[24,9216]{1,0:T(8,128)(2,1)S(1)}, bf16[24,9216]{1,0:T(8,128)(2,1)S(1)}, u32[]{:S(2)}, u32[]{:S(2)}) collective-permute-start(bf16[24,9216]{1,0:T(8,128)(2,1)S(1)} %collective-permute-done.1), channel_id=1, source_target_pairs={{0,28},{4,0},{8,4},{12,8},{16,12},{20,16},{24,20},{28,24},{1,29},{... | collective-permute-start | bytes 1327112 | tf_op jit(solution)/shard_map/ppermute | solution.py:89
  35.7 0.8 constant_dynamic-update-slice_fusion.13
  36.5 5.8 %collective-permute-done.2 = bf16[24,9216]{1,0:T(8,128)(2,1)S(1)} collective-permute-done((bf16[24,9216]{1,0:T(8,128)(2,1)S(1)}, bf16[24,9216]{1,0:T(8,128)(2,1)S(1)}, u32[]{:S(2)}, u32[]{:S(2)}) %collective-permute-start.2) | collective-permute-done | bytes 442400 | tf_op jit(solution)/shard_map/ppermute | solution.py:89
  42.3 5.2 %collective-permute-start.3 = (bf16[24,9216]{1,0:T(8,128)(2,1)S(1)}, bf16[24,9216]{1,0:T(8,128)(2,1)S(1)}, u32[]{:S(2)}, u32[]{:S(2)}) collective-permute-start(bf16[24,9216]{1,0:T(8,128)(2,1)S(1)} %collective-permute-done.2), channel_id=1, source_target_pairs={{0,28},{4,0},{8,4},{12,8},{16,12},{20,16},{24,20},{28,24},{1,29},{... | collective-permute-start | bytes 1327112 | tf_op jit(solution)/shard_map/ppermute | solution.py:89
  47.5 0.8 constant_dynamic-update-slice_fusion.12
  48.3 5.0 %collective-permute-done.3 = bf16[24,9216]{1,0:T(8,128)(2,1)S(1)} collective-permute-done((bf16[24,9216]{1,0:T(8,128)(2,1)S(1)}, bf16[24,9216]{1,0:T(8,128)(2,1)S(1)}, u32[]{:S(2)}, u32[]{:S(2)}) %collective-permute-start.3) | collective-permute-done | bytes 442400 | tf_op jit(solution)/shard_map/ppermute | solution.py:89
  53.3 5.2 %collective-permute-start.4 = (bf16[24,9216]{1,0:T(8,128)(2,1)S(1)}, bf16[24,9216]{1,0:T(8,128)(2,1)S(1)}, u32[]{:S(2)}, u32[]{:S(2)}) collective-permute-start(bf16[24,9216]{1,0:T(8,128)(2,1)S(1)} %collective-permute-done.3), channel_id=1, source_target_pairs={{0,28},{4,0},{8,4},{12,8},{16,12},{20,16},{24,20},{28,24},{1,29},{... | collective-permute-start | bytes 1327112 | tf_op jit(solution)/shard_map/ppermute | solution.py:89
  58.5 0.8 constant_dynamic-update-slice_fusion.11
  59.3 5.9 %collective-permute-done.4 = bf16[24,9216]{1,0:T(8,128)(2,1)S(1)} collective-permute-done((bf16[24,9216]{1,0:T(8,128)(2,1)S(1)}, bf16[24,9216]{1,0:T(8,128)(2,1)S(1)}, u32[]{:S(2)}, u32[]{:S(2)}) %collective-permute-start.4) | collective-permute-done | bytes 442400 | tf_op jit(solution)/shard_map/ppermute | solution.py:89
  65.1 5.2 %collective-permute-start.5 = (bf16[24,9216]{1,0:T(8,128)(2,1)S(1)}, bf16[24,9216]{1,0:T(8,128)(2,1)S(1)}, u32[]{:S(2)}, u32[]{:S(2)}) collective-permute-start(bf16[24,9216]{1,0:T(8,128)(2,1)S(1)} %collective-permute-done.4), channel_id=1, source_target_pairs={{0,28},{4,0},{8,4},{12,8},{16,12},{20,16},{24,20},{28,24},{1,29},{... | collective-permute-start | bytes 1327112 | tf_op jit(solution)/shard_map/ppermute | solution.py:89
  70.3 0.8 constant_dynamic-update-slice_fusion.10
  71.1 7.0 %collective-permute-done.5 = bf16[24,9216]{1,0:T(8,128)(2,1)S(1)} collective-permute-done((bf16[24,9216]{1,0:T(8,128)(2,1)S(1)}, bf16[24,9216]{1,0:T(8,128)(2,1)S(1)}, u32[]{:S(2)}, u32[]{:S(2)}) %collective-permute-start.5) | collective-permute-done | bytes 442400 | tf_op jit(solution)/shard_map/ppermute | solution.py:89
  78.1 5.2 %collective-permute-start.6 = (bf16[24,9216]{1,0:T(8,128)(2,1)S(1)}, bf16[24,9216]{1,0:T(8,128)(2,1)S(1)}, u32[]{:S(2)}, u32[]{:S(2)}) collective-permute-start(bf16[24,9216]{1,0:T(8,128)(2,1)S(1)} %collective-permute-done.5), channel_id=1, source_target_pairs={{0,28},{4,0},{8,4},{12,8},{16,12},{20,16},{24,20},{28,24},{1,29},{... | collective-permute-start | bytes 1327112 | tf_op jit(solution)/shard_map/ppermute | solution.py:89
  83.3 0.8 constant_dynamic-update-slice_fusion.9
  84.1 5.0 %collective-permute-done.6 = bf16[24,9216]{1,0:T(8,128)(2,1)S(1)} collective-permute-done((bf16[24,9216]{1,0:T(8,128)(2,1)S(1)}, bf16[24,9216]{1,0:T(8,128)(2,1)S(1)}, u32[]{:S(2)}, u32[]{:S(2)}) %collective-permute-start.6) | collective-permute-done | bytes 442400 | tf_op jit(solution)/shard_map/ppermute | solution.py:89
  89.1 0.8 constant_dynamic-update-slice_fusion.8
  89.9 0.8 constant_dynamic-update-slice_fusion.7
  90.7 0.8 constant_dynamic-update-slice_fusion.6
  91.5 0.8 constant_dynamic-update-slice_fusion.5
  92.3 0.8 constant_dynamic-update-slice_fusion.4
  93.1 0.8 constant_dynamic-update-slice_fusion.3
  93.9 0.8 constant_dynamic-update-slice_fusion.2
  94.7 0.8 constant_dynamic-update-slice_fusion.1
  95.5 0.8 constant_dynamic-update-slice_fusion
  96.3 9.6 %fusion.31 = (f32[192]{0:T(256)S(1)}, f32[192,1024]{1,0:T(8,128)S(1)}) fusion(bf16[9216,1024]{1,0:T(8,128)(2,1)} %param.8, bf16[384,9216]{1,0:T(8,128)(2,1)} %constant_dynamic-update-slice_fusion, s32[]{:T(128)S(6)} %select_n.37), kind=kOutput, calls=%fused_computation.67 | convolution fusion | flops 3624075008 | bytes 23200516 | tf_op jit(solution)/shard_map/dot_general | solution.py:101
  106.0 8.6 %fusion.30 = (f32[192]{0:T(256)S(1)}, f32[192,1024]{1,0:T(8,128)S(1)}) fusion(bf16[9216,1024]{1,0:T(8,128)(2,1)} %param.7, bf16[384,9216]{1,0:T(8,128)(2,1)S(1)} %copy-done.1, s32[]{:T(128)S(6)} %select_n.37), kind=kOutput, calls=%fused_computation.66 | convolution fusion | flops 3624075008 | bytes 23200516 | tf_op jit(solution)/shard_map/dot_general | solution.py:100
  114.6 0.7 multiply_reduce_fusion
  115.3 0.7 all_to_all.60
  116.0 6.5 %all-to-all-start.3 = ((f32[8,1,24]{2,1,0:T(1,128)}), f32[8,1,24]{2,1,0:T(1,128)S(1)}, u32[]{:S(2)}, u32[]{:S(2)}) async-start(f32[8,1,24]{2,1,0:T(1,128)} %all_to_all.60), calls=%async_computation.3 | async-start | bytes 8192 | tf_op jit(solution)/shard_map/all_to_all | solution.py:113
  122.5 0.7 all_to_all.54
  123.2 5.8 %all-to-all-done.3 = f32[8,1,24]{2,1,0:T(1,128)S(1)} async-done(((f32[8,1,24]{2,1,0:T(1,128)}), f32[8,1,24]{2,1,0:T(1,128)S(1)}, u32[]{:S(2)}, u32[]{:S(2)}) %all-to-all-start.3) | async-done | bytes 800 | tf_op jit(solution)/shard_map/all_to_all | solution.py:113
  129.0 3.3 %all-to-all-start.1 = ((f32[8,1,24]{2,1,0:T(1,128)}), f32[8,1,24]{2,1,0:T(1,128)S(1)}, u32[]{:S(2)}, u32[]{:S(2)}) async-start(f32[8,1,24]{2,1,0:T(1,128)} %all_to_all.54), calls=%async_computation.1 | async-start | bytes 8192 | tf_op jit(solution)/shard_map/all_to_all | solution.py:113
  132.3 0.7 all_to_all.64
  133.0 5.8 %all-to-all-done.1 = f32[8,1,24]{2,1,0:T(1,128)S(1)} async-done(((f32[8,1,24]{2,1,0:T(1,128)}), f32[8,1,24]{2,1,0:T(1,128)S(1)}, u32[]{:S(2)}, u32[]{:S(2)}) %all-to-all-start.1) | async-done | bytes 800 | tf_op jit(solution)/shard_map/all_to_all | solution.py:113
  138.7 3.3 %all-to-all-start.4 = ((f32[8,1,24]{2,1,0:T(1,128)}), f32[8,1,24]{2,1,0:T(1,128)S(1)}, u32[]{:S(2)}, u32[]{:S(2)}) async-start(f32[8,1,24]{2,1,0:T(1,128)} %all_to_all.64), calls=%async_computation.4 | async-start | bytes 8192 | tf_op jit(solution)/shard_map/all_to_all | solution.py:113
  142.0 0.7 all_to_all.52
  142.7 5.7 %all-to-all-done.4 = f32[8,1,24]{2,1,0:T(1,128)S(1)} async-done(((f32[8,1,24]{2,1,0:T(1,128)}), f32[8,1,24]{2,1,0:T(1,128)S(1)}, u32[]{:S(2)}, u32[]{:S(2)}) %all-to-all-start.4) | async-done | bytes 800 | tf_op jit(solution)/shard_map/all_to_all | solution.py:113
  148.5 3.2 %all-to-all-start = ((f32[8,1,24]{2,1,0:T(1,128)}), f32[8,1,24]{2,1,0:T(1,128)S(1)}, u32[]{:S(2)}, u32[]{:S(2)}) async-start(f32[8,1,24]{2,1,0:T(1,128)} %all_to_all.52), calls=%async_computation | async-start | bytes 8192 | tf_op jit(solution)/shard_map/all_to_all | solution.py:113
  151.7 0.7 all_to_all.56
  152.4 5.7 %all-to-all-done = f32[8,1,24]{2,1,0:T(1,128)S(1)} async-done(((f32[8,1,24]{2,1,0:T(1,128)}), f32[8,1,24]{2,1,0:T(1,128)S(1)}, u32[]{:S(2)}, u32[]{:S(2)}) %all-to-all-start) | async-done | bytes 800 | tf_op jit(solution)/shard_map/all_to_all | solution.py:113
  158.1 3.3 %all-to-all-start.2 = ((f32[8,1,24]{2,1,0:T(1,128)}), f32[8,1,24]{2,1,0:T(1,128)S(1)}, u32[]{:S(2)}, u32[]{:S(2)}) async-start(f32[8,1,24]{2,1,0:T(1,128)} %all_to_all.56), calls=%async_computation.2 | async-start | bytes 8192 | tf_op jit(solution)/shard_map/all_to_all | solution.py:113
  161.5 0.6 dynamic-slice
  162.7 0.7 all_to_all.67
  163.4 0.7 all_to_all.69
  164.1 3.8 %all-to-all-done.2 = f32[8,1,24]{2,1,0:T(1,128)S(1)} async-done(((f32[8,1,24]{2,1,0:T(1,128)}), f32[8,1,24]{2,1,0:T(1,128)S(1)}, u32[]{:S(2)}, u32[]{:S(2)}) %all-to-all-start.2) | async-done | bytes 800 | tf_op jit(solution)/shard_map/all_to_all | solution.py:113
  167.9 3.2 %all-to-all-start.5 = ((f32[8,1,24]{2,1,0:T(1,128)}), f32[8,1,24]{2,1,0:T(1,128)S(1)}, u32[]{:S(2)}, u32[]{:S(2)}) async-start(f32[8,1,24]{2,1,0:T(1,128)} %all_to_all.67), calls=%async_computation.5 | async-start | bytes 8192 | tf_op jit(solution)/shard_map/all_to_all | solution.py:113
  171.2 6.4 %all-to-all-done.5 = f32[8,1,24]{2,1,0:T(1,128)S(1)} async-done(((f32[8,1,24]{2,1,0:T(1,128)}), f32[8,1,24]{2,1,0:T(1,128)S(1)}, u32[]{:S(2)}, u32[]{:S(2)}) %all-to-all-start.5) | async-done | bytes 800 | tf_op jit(solution)/shard_map/all_to_all | solution.py:113
  177.6 3.3 %all-to-all-start.6 = ((f32[8,1,24]{2,1,0:T(1,128)}), f32[8,1,24]{2,1,0:T(1,128)S(1)}, u32[]{:S(2)}, u32[]{:S(2)}) async-start(f32[8,1,24]{2,1,0:T(1,128)} %all_to_all.69), calls=%async_computation.6 | async-start | bytes 8192 | tf_op jit(solution)/shard_map/all_to_all | solution.py:113
  180.9 0.2 dynamic-update-slice.1
  181.2 0.2 dynamic-update-slice
  182.0 0.2 dynamic-update-slice.6
  182.2 5.1 %all-to-all-done.6 = f32[8,1,24]{2,1,0:T(1,128)S(1)} async-done(((f32[8,1,24]{2,1,0:T(1,128)}), f32[8,1,24]{2,1,0:T(1,128)S(1)}, u32[]{:S(2)}, u32[]{:S(2)}) %all-to-all-start.6) | async-done | bytes 800 | tf_op jit(solution)/shard_map/all_to_all | solution.py:113
  187.3 0.2 dynamic-update-slice.7
  187.6 5.6 %all-reduce.8 = (f32[96]{0:T(128)S(1)}, f32[96]{0:T(128)S(1)}, f32[96]{0:T(128)S(1)}, f32[96]{0:T(128)S(1)}, f32[96]{0:T(128)S(1)}, /*index=5*/f32[96]{0:T(128)S(1)}, f32[96]{0:T(128)S(1)}) all-reduce(f32[96]{0:T(128)S(1)} %dynamic-update-slice, f32[96]{0:T(128)S(1)} %dynamic-update-slice.1, ...), channel_id=2, replica_groups=mesh['tok'=8,'vocab'=4] {'vocab'}, use_global_device_ids=true, to_apply=%add | all-reduce | flops 672 | bytes 5376
  193.8 0.3 while.27
  194.1 0.5 subtract_add_fusion
  (44 shorter events, 1.6 us)
Async XLA Ops:
  0.6 89.3 %copy-start = (bf16[24,9216]{1,0:T(8,128)(2,1)S(1)}, bf16[24,9216]{1,0:T(8,128)(2,1)}, u32[]{:S(2)}) copy-start(bf16[24,9216]{1,0:T(8,128)(2,1)} %param.6) | copy-start | bytes 1327108
  0.6 21.1 %collective-permute-start = (bf16[24,9216]{1,0:T(8,128)(2,1)}, bf16[24,9216]{1,0:T(8,128)(2,1)S(1)}, u32[]{:S(2)}, u32[]{:S(2)}) collective-permute-start(bf16[24,9216]{1,0:T(8,128)(2,1)} %param.6), channel_id=1, source_target_pairs={{0,28},{4,0},{8,4},{12,8},{16,12},{20,16},{24,20},{28,24},{1,29},{... | collective-permute-start | bytes 1327112 | tf_op jit(solution)/shard_map/ppermute | solution.py:89
  21.8 10.3 %collective-permute-start.1 = (bf16[24,9216]{1,0:T(8,128)(2,1)S(1)}, bf16[24,9216]{1,0:T(8,128)(2,1)S(1)}, u32[]{:S(2)}, u32[]{:S(2)}) collective-permute-start(bf16[24,9216]{1,0:T(8,128)(2,1)S(1)} %collective-permute-done), channel_id=1, source_target_pairs={{0,28},{4,0},{8,4},{12,8},{16,12},{20,16},{24,20},{28,24},{1,29},{... | collective-permute-start | bytes 1327112 | tf_op jit(solution)/shard_map/ppermute | solution.py:89
  32.1 10.2 %collective-permute-start.2 = (bf16[24,9216]{1,0:T(8,128)(2,1)S(1)}, bf16[24,9216]{1,0:T(8,128)(2,1)S(1)}, u32[]{:S(2)}, u32[]{:S(2)}) collective-permute-start(bf16[24,9216]{1,0:T(8,128)(2,1)S(1)} %collective-permute-done.1), channel_id=1, source_target_pairs={{0,28},{4,0},{8,4},{12,8},{16,12},{20,16},{24,20},{28,24},{1,29},{... | collective-permute-start | bytes 1327112 | tf_op jit(solution)/shard_map/ppermute | solution.py:89
  42.3 11.0 %collective-permute-start.3 = (bf16[24,9216]{1,0:T(8,128)(2,1)S(1)}, bf16[24,9216]{1,0:T(8,128)(2,1)S(1)}, u32[]{:S(2)}, u32[]{:S(2)}) collective-permute-start(bf16[24,9216]{1,0:T(8,128)(2,1)S(1)} %collective-permute-done.2), channel_id=1, source_target_pairs={{0,28},{4,0},{8,4},{12,8},{16,12},{20,16},{24,20},{28,24},{1,29},{... | collective-permute-start | bytes 1327112 | tf_op jit(solution)/shard_map/ppermute | solution.py:89
  53.3 11.8 %collective-permute-start.4 = (bf16[24,9216]{1,0:T(8,128)(2,1)S(1)}, bf16[24,9216]{1,0:T(8,128)(2,1)S(1)}, u32[]{:S(2)}, u32[]{:S(2)}) collective-permute-start(bf16[24,9216]{1,0:T(8,128)(2,1)S(1)} %collective-permute-done.3), channel_id=1, source_target_pairs={{0,28},{4,0},{8,4},{12,8},{16,12},{20,16},{24,20},{28,24},{1,29},{... | collective-permute-start | bytes 1327112 | tf_op jit(solution)/shard_map/ppermute | solution.py:89
  65.1 13.0 %collective-permute-start.5 = (bf16[24,9216]{1,0:T(8,128)(2,1)S(1)}, bf16[24,9216]{1,0:T(8,128)(2,1)S(1)}, u32[]{:S(2)}, u32[]{:S(2)}) collective-permute-start(bf16[24,9216]{1,0:T(8,128)(2,1)S(1)} %collective-permute-done.4), channel_id=1, source_target_pairs={{0,28},{4,0},{8,4},{12,8},{16,12},{20,16},{24,20},{28,24},{1,29},{... | collective-permute-start | bytes 1327112 | tf_op jit(solution)/shard_map/ppermute | solution.py:89
  78.1 11.0 %collective-permute-start.6 = (bf16[24,9216]{1,0:T(8,128)(2,1)S(1)}, bf16[24,9216]{1,0:T(8,128)(2,1)S(1)}, u32[]{:S(2)}, u32[]{:S(2)}) collective-permute-start(bf16[24,9216]{1,0:T(8,128)(2,1)S(1)} %collective-permute-done.5), channel_id=1, source_target_pairs={{0,28},{4,0},{8,4},{12,8},{16,12},{20,16},{24,20},{28,24},{1,29},{... | collective-permute-start | bytes 1327112 | tf_op jit(solution)/shard_map/ppermute | solution.py:89
  96.3 9.6 %copy-start.1 = (bf16[384,9216]{1,0:T(8,128)(2,1)S(1)}, bf16[384,9216]{1,0:T(8,128)(2,1)}, u32[]{:S(2)}) copy-start(bf16[384,9216]{1,0:T(8,128)(2,1)} %constant_dynamic-update-slice_fusion) | copy-start | bytes 21233668
  106.0 55.5 %copy-start.2 = (u32[32]{0:T(128)S(1)}, u32[32]{0:T(128)}, u32[]{:S(2)}) copy-start(u32[32]{0:T(128)} %constant.77) | copy-start | bytes 388
  116.0 13.0 %all-to-all-start.3 = ((f32[8,1,24]{2,1,0:T(1,128)}), f32[8,1,24]{2,1,0:T(1,128)S(1)}, u32[]{:S(2)}, u32[]{:S(2)}) async-start(f32[8,1,24]{2,1,0:T(1,128)} %all_to_all.60), calls=%async_computation.3 | async-start | bytes 8192 | tf_op jit(solution)/shard_map/all_to_all | solution.py:113
  129.0 9.8 %all-to-all-start.1 = ((f32[8,1,24]{2,1,0:T(1,128)}), f32[8,1,24]{2,1,0:T(1,128)S(1)}, u32[]{:S(2)}, u32[]{:S(2)}) async-start(f32[8,1,24]{2,1,0:T(1,128)} %all_to_all.54), calls=%async_computation.1 | async-start | bytes 8192 | tf_op jit(solution)/shard_map/all_to_all | solution.py:113
  138.7 9.7 %all-to-all-start.4 = ((f32[8,1,24]{2,1,0:T(1,128)}), f32[8,1,24]{2,1,0:T(1,128)S(1)}, u32[]{:S(2)}, u32[]{:S(2)}) async-start(f32[8,1,24]{2,1,0:T(1,128)} %all_to_all.64), calls=%async_computation.4 | async-start | bytes 8192 | tf_op jit(solution)/shard_map/all_to_all | solution.py:113
  148.5 9.7 %all-to-all-start = ((f32[8,1,24]{2,1,0:T(1,128)}), f32[8,1,24]{2,1,0:T(1,128)S(1)}, u32[]{:S(2)}, u32[]{:S(2)}) async-start(f32[8,1,24]{2,1,0:T(1,128)} %all_to_all.52), calls=%async_computation | async-start | bytes 8192 | tf_op jit(solution)/shard_map/all_to_all | solution.py:113
  158.1 9.8 %all-to-all-start.2 = ((f32[8,1,24]{2,1,0:T(1,128)}), f32[8,1,24]{2,1,0:T(1,128)S(1)}, u32[]{:S(2)}, u32[]{:S(2)}) async-start(f32[8,1,24]{2,1,0:T(1,128)} %all_to_all.56), calls=%async_computation.2 | async-start | bytes 8192 | tf_op jit(solution)/shard_map/all_to_all | solution.py:113
  167.9 9.7 %all-to-all-start.5 = ((f32[8,1,24]{2,1,0:T(1,128)}), f32[8,1,24]{2,1,0:T(1,128)S(1)}, u32[]{:S(2)}, u32[]{:S(2)}) async-start(f32[8,1,24]{2,1,0:T(1,128)} %all_to_all.67), calls=%async_computation.5 | async-start | bytes 8192 | tf_op jit(solution)/shard_map/all_to_all | solution.py:113
  177.6 9.7 %all-to-all-start.6 = ((f32[8,1,24]{2,1,0:T(1,128)}), f32[8,1,24]{2,1,0:T(1,128)S(1)}, u32[]{:S(2)}, u32[]{:S(2)}) async-start(f32[8,1,24]{2,1,0:T(1,128)} %all_to_all.69), calls=%async_computation.6 | async-start | bytes 8192 | tf_op jit(solution)/shard_map/all_to_all | solution.py:113
